TPU v7x, 32 devices: a whole 2x2x4 slice. The times are simulated.
32 devices in a mesh: replica: 2 (over x), fsdp: 16 (over z, y, core).
Axes of the slice: x: 2, y: 2, z: 4, core: 2. Of those that a mesh axis runs over, the one named last changes fastest.
Arguments:
- tokens: bfloat16 [16384, 1152], P(('replica', 'fsdp')), may hold values from -6 to 6
- cotangent: bfloat16 [16384, 1152], P(('replica', 'fsdp')), may hold values from -6 to 6
- piece_starts: int32 [32, 1], P(('replica', 'fsdp')), may hold values from 0 to 256, as said below
- w_query: bfloat16 [1152, 1024], P('fsdp'), may hold values from -0.1875 to 0.1875
- w_key: bfloat16 [1152, 256], P('fsdp'), may hold values from -0.1875 to 0.1875
- w_value: bfloat16 [1152, 256], P('fsdp'), may hold values from -0.1875 to 0.1875
- w_out: bfloat16 [1024, 1152], P('fsdp'), may hold values from -0.1875 to 0.1875
- w_gate: bfloat16 [1152, 6912], P('fsdp'), may hold values from -0.1875 to 0.1875
- w_up: bfloat16 [1152, 6912], P('fsdp'), may hold values from -0.1875 to 0.1875
- w_down: bfloat16 [6912, 1152], P('fsdp'), may hold values from -0.078125 to 0.078125
- attn_pre_gain: bfloat16 [1152], P('fsdp'), may hold values from 0.5 to 1.5
- query_gain: bfloat16 [256], P('fsdp'), may hold values from 1 to 2.5
- key_gain: bfloat16 [256], P('fsdp'), may hold values from 0.25 to 1.75
- attn_post_gain: bfloat16 [1152], P('fsdp'), may hold values from 0.25 to 1.75
- mlp_pre_gain: bfloat16 [1152], P('fsdp'), may hold values from 0.5 to 1.5
- mlp_post_gain: bfloat16 [1152], P('fsdp'), may hold values from 0.25 to 1.75
Outputs:
- layer_out: bfloat16 [16384, 1152], P(('replica', 'fsdp'))
- input_grad: float32 [16384, 1152], P(('replica', 'fsdp'))
- grad_query: float32 [1152, 1024], P('fsdp')
- grad_key: float32 [1152, 256], P('fsdp')
- grad_value: float32 [1152, 256], P('fsdp')
- grad_out: float32 [1024, 1152], P('fsdp')
- grad_gate: float32 [1152, 6912], P('fsdp')
- grad_up: float32 [1152, 6912], P('fsdp')
- grad_down: float32 [6912, 1152], P('fsdp')
- grad_attn_pre: float32 [1152], P('fsdp')
- grad_query_gain: float32 [256], P('fsdp')
- grad_key_gain: float32 [256], P('fsdp')
- grad_attn_post: float32 [1152], P('fsdp')
- grad_mlp_pre: float32 [1152], P('fsdp')
- grad_mlp_post: float32 [1152], P('fsdp')
Inputs may be any that keep to these rules, and one draw needn't show every extreme that they name: `piece_starts`: each row holds the starts of the 1 image pieces of 256 tokens in one sequence, rising, the pieces disjoint and within the sequence's 512 tokens; the other tokens of the sequence are causal text.
All inputs are finite; a program needn't handle non-finite values.
Results may differ from a plain program's by a relative error of at most 0.018.
Values may be sent and summed in bfloat16 or wider, within the bound.
A program may use at most 320 MiB of HBM per device.

v0:
```python
import jax
import jax.numpy as jnp
from jax import lax
from jax.sharding import PartitionSpec as P

D = 1152
H = 4
HD = 256
FF = 6912
PIECE = 256
epsilon = 1e-06
rope_base = 1000000.0
masked_value = -1e30


def row_scale(values):
    return lax.rsqrt(jnp.mean(values * values, axis=-1, keepdims=True) + epsilon)


def norm_back(values, scale, gain, upstream):
    weighted = upstream * gain
    inner = jnp.mean(weighted * values, axis=-1, keepdims=True)
    grad_values = scale * weighted - values * (scale * scale * scale) * inner
    grad_gain = jnp.sum((upstream * values * scale).reshape(-1, values.shape[-1]), axis=0)
    return (grad_values, grad_gain)


def rope_tables(length, width):
    positions = jnp.arange(length, dtype=jnp.float32)
    freqs = rope_base ** (-jnp.arange(width // 2, dtype=jnp.float32) * 2.0 / width)
    angles = positions[:, None] * freqs[None, :]
    return (jnp.cos(angles), jnp.sin(angles))


def rotate(values, cosine, sine):
    half = values.shape[-1] // 2
    first = values[..., :half]
    second = values[..., half:]
    return jnp.concatenate(
        [first * cosine - second * sine, second * cosine + first * sine], axis=-1
    )


def rotate_back(upstream, cosine, sine):
    half = upstream.shape[-1] // 2
    first = upstream[..., :half]
    second = upstream[..., half:]
    return jnp.concatenate(
        [first * cosine + second * sine, second * cosine - first * sine], axis=-1
    )


def score_mask(rows, columns, starts):
    inside_rows = (rows[None, :] >= starts[:, None]) & (rows[None, :] < starts[:, None] + PIECE)
    inside_cols = (columns[None, :] >= starts[:, None]) & (
        columns[None, :] < starts[:, None] + PIECE
    )
    same = jnp.any(inside_rows[:, :, None] & inside_cols[:, None, :], axis=0)
    return (columns[None, :] <= rows[:, None]) | same


def matmul(left, right):
    return jnp.dot(left, right, preferred_element_type=jnp.float32)


def matmul_back(left, right):
    return lax.dot_general(
        left, right, (((1,), (1,)), ((), ())), preferred_element_type=jnp.float32
    )


def term_maker(left, rights):

    def term(start, count):
        parts = [
            lax.dot_general(
                left, right, (((0,), (0,)), ((), ())), preferred_element_type=jnp.float32
            )
            for right in rights
        ]
        return jnp.concatenate(parts, axis=1)

    return term


def on_device(
    tokens,
    cotangent,
    piece_starts,
    w_query,
    w_key,
    w_value,
    w_out,
    w_gate,
    w_up,
    w_down,
    attn_pre_gain,
    query_gain,
    key_gain,
    attn_post_gain,
    mlp_pre_gain,
    mlp_post_gain,
):
    length = tokens.shape[0]
    starts = piece_starts[0]
    fsdp_count = lax.axis_size("fsdp")
    attn_full = (
        lax.all_gather(w_query, "fsdp", axis=0, tiled=True),
        lax.all_gather(w_key, "fsdp", axis=0, tiled=True),
        lax.all_gather(w_value, "fsdp", axis=0, tiled=True),
        lax.all_gather(w_out, "fsdp", axis=0, tiled=True),
        lax.all_gather(attn_pre_gain, "fsdp", axis=0, tiled=True),
        lax.all_gather(query_gain, "fsdp", axis=0, tiled=True),
        lax.all_gather(key_gain, "fsdp", axis=0, tiled=True),
        lax.all_gather(attn_post_gain, "fsdp", axis=0, tiled=True),
    )
    gain_attn_pre = attn_full[4].astype(jnp.float32)
    gain_query = attn_full[5].astype(jnp.float32)
    gain_key = attn_full[6].astype(jnp.float32)
    gain_attn_post = attn_full[7].astype(jnp.float32)
    inputs = tokens.astype(jnp.float32)
    scale_attn = row_scale(inputs)
    normed_attn = (inputs * scale_attn * gain_attn_pre).astype(jnp.bfloat16)
    query_proj = matmul(normed_attn, attn_full[0]).reshape(length, H, HD)
    key_proj = matmul(normed_attn, attn_full[1])
    value_proj = matmul(normed_attn, attn_full[2])
    cosine, sine = rope_tables(length, HD)
    attn_factor = HD ** (-0.5)
    scale_query = row_scale(query_proj)
    query_low = (
        rotate(query_proj * scale_query * gain_query, cosine[:, None, :], sine[:, None, :])
        * attn_factor
    ).astype(jnp.bfloat16)
    scale_key = row_scale(key_proj)
    key_low = rotate(key_proj * scale_key * gain_key, cosine, sine).astype(jnp.bfloat16)
    value_low = value_proj.astype(jnp.bfloat16)
    count = length // length
    columns = jnp.arange(length, dtype=jnp.int32)
    block_ids = jnp.arange(count, dtype=jnp.int32)
    query_blocks = query_low.reshape(count, length, H, HD)

    def attend(item):
        index, queries = item
        rows = index * length + jnp.arange(length, dtype=jnp.int32)
        allowed = score_mask(rows, columns, starts)
        scores = jnp.einsum("thd,sd->hts", queries, key_low, preferred_element_type=jnp.float32)
        scores = jnp.where(allowed[None], scores, masked_value)
        peak = jnp.max(scores, axis=-1, keepdims=True)
        expo = jnp.exp(scores - peak)
        total = jnp.sum(expo, axis=-1, keepdims=True)
        probs_low = (expo / total).astype(jnp.bfloat16)
        mixed_part = jnp.einsum(
            "hts,sd->thd", probs_low, value_low, preferred_element_type=jnp.float32
        )
        return (mixed_part, (peak + jnp.log(total))[..., 0])

    mixed_parts, logsums = lax.map(attend, (block_ids, query_blocks))
    mixed_low = mixed_parts.reshape(length, H * HD).astype(jnp.bfloat16)
    attn_out = matmul(mixed_low, attn_full[3])
    scale_post = row_scale(attn_out)
    resid = inputs + attn_out * scale_post * gain_attn_post
    mlp_full = (
        lax.all_gather(w_gate, "fsdp", axis=0, tiled=True),
        lax.all_gather(w_up, "fsdp", axis=0, tiled=True),
        lax.all_gather(w_down, "fsdp", axis=0, tiled=True),
        lax.all_gather(mlp_pre_gain, "fsdp", axis=0, tiled=True),
        lax.all_gather(mlp_post_gain, "fsdp", axis=0, tiled=True),
    )
    gain_mlp_pre = mlp_full[3].astype(jnp.float32)
    gain_mlp_post = mlp_full[4].astype(jnp.float32)
    scale_mlp = row_scale(resid)
    normed_mlp = (resid * scale_mlp * gain_mlp_pre).astype(jnp.bfloat16)
    gate = matmul(normed_mlp, mlp_full[0])
    upper = matmul(normed_mlp, mlp_full[1])
    activated, gelu_pull = jax.vjp(lambda values: jax.nn.gelu(values, approximate=True), gate)
    hidden_low = (activated * upper).astype(jnp.bfloat16)
    mlp_out = matmul(hidden_low, mlp_full[2])
    scale_out = row_scale(mlp_out)
    layer_out = (resid + mlp_out * scale_out * gain_mlp_post).astype(jnp.bfloat16)
    upstream = cotangent.astype(jnp.float32)
    grad_mlp_out, grad_mlp_post = norm_back(mlp_out, scale_out, gain_mlp_post, upstream)
    grad_mlp_low = grad_mlp_out.astype(jnp.bfloat16)
    grad_hidden = matmul_back(grad_mlp_low, mlp_full[2])
    grad_gate_low = gelu_pull(grad_hidden * upper)[0].astype(jnp.bfloat16)
    grad_up_low = (grad_hidden * activated).astype(jnp.bfloat16)
    grad_normed_mlp = matmul_back(grad_gate_low, mlp_full[0]) + matmul_back(
        grad_up_low, mlp_full[1]
    )
    grad_resid_part, grad_mlp_pre = norm_back(resid, scale_mlp, gain_mlp_pre, grad_normed_mlp)
    grad_resid = upstream + grad_resid_part
    mlp_in_term = term_maker(normed_mlp, (grad_gate_low, grad_up_low))
    down_term = term_maker(hidden_low, (grad_mlp_low,))
    mlp_in_share = lax.psum_scatter(
        mlp_in_term(jnp.int32(0), lax.axis_size("fsdp") * (D // fsdp_count)),
        "fsdp",
        scatter_dimension=0,
        tiled=True,
    )
    down_share = lax.psum_scatter(
        down_term(jnp.int32(0), lax.axis_size("fsdp") * (FF // fsdp_count)),
        "fsdp",
        scatter_dimension=0,
        tiled=True,
    )
    grad_attn_out, grad_attn_post = norm_back(attn_out, scale_post, gain_attn_post, grad_resid)
    grad_attn_low = grad_attn_out.astype(jnp.bfloat16)
    grad_mixed_low = matmul_back(grad_attn_low, attn_full[3]).astype(jnp.bfloat16)
    grad_blocks = grad_mixed_low.reshape(count, length, H, HD)

    def attend_back(carry, item):
        key_total, value_total = carry
        index, queries, grads, logsum = item
        rows = index * length + jnp.arange(length, dtype=jnp.int32)
        allowed = score_mask(rows, columns, starts)
        scores = jnp.einsum("thd,sd->hts", queries, key_low, preferred_element_type=jnp.float32)
        scores = jnp.where(allowed[None], scores, masked_value)
        probs = jnp.exp(scores - logsum[..., None])
        probs_low = probs.astype(jnp.bfloat16)
        grad_probs = jnp.einsum("thd,sd->hts", grads, value_low, preferred_element_type=jnp.float32)
        value_total = value_total + jnp.einsum(
            "hts,thd->sd", probs_low, grads, preferred_element_type=jnp.float32
        )
        inner = jnp.sum(probs * grad_probs, axis=-1, keepdims=True)
        grad_scores = (probs * (grad_probs - inner)).astype(jnp.bfloat16)
        grad_queries = jnp.einsum(
            "hts,sd->thd", grad_scores, key_low, preferred_element_type=jnp.float32
        )
        key_total = key_total + jnp.einsum(
            "hts,thd->sd", grad_scores, queries, preferred_element_type=jnp.float32
        )
        return ((key_total, value_total), grad_queries)

    zero_rows = jnp.zeros((length, HD), jnp.float32)
    (grad_key_rot, grad_value_act), grad_query_parts = lax.scan(
        attend_back, (zero_rows, zero_rows), (block_ids, query_blocks, grad_blocks, logsums)
    )
    grad_query_act = grad_query_parts.reshape(length, H, HD)
    grad_query_normed = rotate_back(
        grad_query_act * attn_factor, cosine[:, None, :], sine[:, None, :]
    )
    grad_query_proj, grad_query_gain = norm_back(
        query_proj, scale_query, gain_query, grad_query_normed
    )
    grad_key_normed = rotate_back(grad_key_rot, cosine, sine)
    grad_key_proj, grad_key_gain = norm_back(key_proj, scale_key, gain_key, grad_key_normed)
    grad_query_low = grad_query_proj.reshape(length, H * HD).astype(jnp.bfloat16)
    grad_key_low = grad_key_proj.astype(jnp.bfloat16)
    grad_value_low = grad_value_act.astype(jnp.bfloat16)
    grad_normed_attn = (
        matmul_back(grad_query_low, attn_full[0])
        + matmul_back(grad_key_low, attn_full[1])
        + matmul_back(grad_value_low, attn_full[2])
    )
    grad_input_part, grad_attn_pre = norm_back(inputs, scale_attn, gain_attn_pre, grad_normed_attn)
    input_grad = grad_resid + grad_input_part
    attn_in_term = term_maker(normed_attn, (grad_query_low, grad_key_low, grad_value_low))
    out_term = term_maker(mixed_low, (grad_attn_low,))
    attn_in_share = lax.psum_scatter(
        attn_in_term(jnp.int32(0), lax.axis_size("fsdp") * (D // fsdp_count)),
        "fsdp",
        scatter_dimension=0,
        tiled=True,
    )
    out_share = lax.psum_scatter(
        out_term(jnp.int32(0), lax.axis_size("fsdp") * (H * HD // fsdp_count)),
        "fsdp",
        scatter_dimension=0,
        tiled=True,
    )
    gains_all = lax.psum(
        (
            grad_attn_pre,
            grad_query_gain,
            grad_key_gain,
            grad_attn_post,
            grad_mlp_pre,
            grad_mlp_post,
        ),
        ("replica", "fsdp"),
    )
    owner = lax.axis_index("fsdp")
    d_rows = D // fsdp_count
    h_rows = HD // fsdp_count
    gain_shares = (
        lax.dynamic_slice_in_dim(gains_all[0], owner * d_rows, d_rows, 0),
        lax.dynamic_slice_in_dim(gains_all[1], owner * h_rows, h_rows, 0),
        lax.dynamic_slice_in_dim(gains_all[2], owner * h_rows, h_rows, 0),
        lax.dynamic_slice_in_dim(gains_all[3], owner * d_rows, d_rows, 0),
        lax.dynamic_slice_in_dim(gains_all[4], owner * d_rows, d_rows, 0),
        lax.dynamic_slice_in_dim(gains_all[5], owner * d_rows, d_rows, 0),
    )
    results = (
        lax.psum(attn_in_share.astype(jnp.bfloat16), "replica").astype(jnp.float32),
        lax.psum(out_share.astype(jnp.bfloat16), "replica").astype(jnp.float32),
        lax.psum(mlp_in_share.astype(jnp.bfloat16), "replica").astype(jnp.float32),
        lax.psum(down_share.astype(jnp.bfloat16), "replica").astype(jnp.float32),
    )
    attn_in_full = results[0]
    mlp_in_full = results[2]
    qwidth = H * HD
    grad_query = attn_in_full[:, :qwidth]
    grad_key = attn_in_full[:, qwidth : qwidth + HD]
    grad_value = attn_in_full[:, qwidth + HD :]
    grad_gate = mlp_in_full[:, :FF]
    grad_up = mlp_in_full[:, FF:]
    return (
        layer_out,
        input_grad,
        grad_query,
        grad_key,
        grad_value,
        results[1],
        grad_gate,
        grad_up,
        results[3],
        gain_shares[0],
        gain_shares[1],
        gain_shares[2],
        gain_shares[3],
        gain_shares[4],
        gain_shares[5],
    )


def solution(mesh):
    placed = (
        P(("replica", "fsdp"), None),
        P(("replica", "fsdp"), None),
        P(("replica", "fsdp"), None),
        P("fsdp", None),
        P("fsdp", None),
        P("fsdp", None),
        P("fsdp", None),
        P("fsdp", None),
        P("fsdp", None),
        P("fsdp", None),
        P("fsdp"),
        P("fsdp"),
        P("fsdp"),
        P("fsdp"),
        P("fsdp"),
        P("fsdp"),
    )
    return jax.shard_map(
        on_device,
        mesh=mesh,
        in_specs=placed,
        out_specs=(
            P(("replica", "fsdp"), None),
            P(("replica", "fsdp"), None),
            P("fsdp", None),
            P("fsdp", None),
            P("fsdp", None),
            P("fsdp", None),
            P("fsdp", None),
            P("fsdp", None),
            P("fsdp", None),
            P("fsdp"),
            P("fsdp"),
            P("fsdp"),
            P("fsdp"),
            P("fsdp"),
            P("fsdp"),
        ),
        check_vma=False,
    )
```

profile of v0, /device:TPU:0, one launch (start us, length us, event | category | flops | bytes accessed | tf_op | source)
XLA Modules:
  0.0 1775.8 jit_solution(9544685377612976665)
XLA Ops:
  14.8 63.6 %all-reduce.8 = (bf16[1152]{0:T(1024)(128)(2,1)S(1)}, bf16[256]{0:T(256)(128)(2,1)S(1)}, bf16[256]{0:T(256)(128)(2,1)S(1)}, bf16[1152]{0:T(1024)(128)(2,1)S(1)},...) all-reduce(bf16[1152]{0:T(1024)(128)(2,1)S(1)} %dynamic-update-slic, ...), channel_id=1, replica_groups=mesh['replica'=2,'fsdp'=16] {'fsdp'}, use_global_device_ids=true, to_apply=%add | all-reduce | flops 5120 | bytes 20480
  81.0 21.2 %all_gather.41 = bf16[1152,256]{1,0:T(8,128)(2,1)S(1)} all-gather(bf16[72,256]{1,0:T(8,128)(2,1)S(1)} %copy-done.69), channel_id=1, replica_groups=mesh['replica'=2,'fsdp'=16] {'fsdp'}, dimensions={0}, use_global_device_ids=true | all-gather | bytes 626688 | tf_op jit(solution)/shard_map/all_gather | solution.py:109
  108.0 21.2 %all_gather.40 = bf16[1152,256]{1,0:T(8,128)(2,1)S(1)} all-gather(bf16[72,256]{1,0:T(8,128)(2,1)S(1)} %copy-done.70), channel_id=1, replica_groups=mesh['replica'=2,'fsdp'=16] {'fsdp'}, dimensions={0}, use_global_device_ids=true | all-gather | bytes 626688 | tf_op jit(solution)/shard_map/all_gather | solution.py:110
  153.9 71.6 %all-gather.10.cloned.1.call-done = bf16[1152,6912]{1,0:T(8,128)(2,1)} async-done(((bf16[72,6912]{1,0:T(8,128)(2,1)}), bf16[1152,6912]{1,0:T(8,128)(2,1)}) %all-gather.10.cloned.1.call-update) | async-done | bytes 15925264 | tf_op jit(solution)/shard_map/all_gather | solution.py:163
  225.6 16.0 fusion.86
  241.5 105.8 %all-gather.12.cloned.1.call-done = bf16[1152,6912]{1,0:T(8,128)(2,1)} async-done(((bf16[72,6912]{1,0:T(8,128)(2,1)}), bf16[1152,6912]{1,0:T(8,128)(2,1)}) %all-gather.12.cloned.1.call-update) | async-done | bytes 15925264 | tf_op jit(solution)/shard_map/all_gather | solution.py:164
  347.3 21.5 %multiply_convert_fusion.1 = (bf16[512,6912]{1,0:T(8,128)(2,1)}, f32[512,6912]{1,0:T(8,128)}) fusion(f32[512,6912]{1,0:T(8,128)} %fusion.86, bf16[512,1152]{1,0:T(8,128)(2,1)S(1)} %multiply_convert_fusion.2, bf16[1152,6912]{1,0:T(8,128)(2,1)} %all-gather.12.cloned.1.call-done), kind=kOutput, calls=%fused_computation.11 | convolution fusion | flops 8189116416 | bytes 52494336 | tf_op jit(solution)/shard_map/dot_general | solution.py:63
  368.8 100.3 %all-gather.14.cloned.1.call-done = bf16[6912,1152]{1,0:T(8,128)(2,1)} async-done(((bf16[432,1152]{1,0:T(8,128)(2,1)}), bf16[6912,1152]{1,0:T(8,128)(2,1)}) %all-gather.14.cloned.1.call-update) | async-done | bytes 15925264 | tf_op jit(solution)/shard_map/all_gather | solution.py:165
  469.1 14.5 multiply_reduce_fusion.4
  487.3 28.6 %multiply_convert_fusion = (bf16[512,6912]{1,0:T(8,128)(2,1)}, bf16[512,6912]{1,0:T(8,128)(2,1)}) fusion(f32[512,6912]{1,0:T(8,128)} %fusion.86, f32[512,6912]{1,0:T(8,128)} %get-tuple-element.216, bf16[6912,1152]{1,0:T(8,128)(2,1)} %all-gather.14.cloned.1.call-done, bf16[512,1152]{1,0:T(8,128)(2,1)S(1)} %copy-done.26, f32[512,1152]{1,0:T(8,128)} %copy-done.33, ...), kind=kOutput, calls=%fused_computation.10 | convolution fusion | flops 8242790400 | bytes 61942272 | tf_op jit(solution)/shard_map/dot_general | solution.py:67
  515.9 15.7 fusion.87
  531.7 16.0 multiply_reduce_fusion
  587.4 3.9 fusion.77
  591.3 5.7 pad_maximum_fusion.1
  597.0 8.1 copy.151
  605.8 18.6 %fusion.69 = f32[6912,1152]{1,0:T(8,128)} fusion(bf16[512,6912]{1,0:T(8,128)(2,1)} %get-tuple-element.215, bf16[512,1152]{1,0:T(8,128)(2,1)} %param.17, f32[512,1152]{1,0:T(8,128)} %copy-done.33, f32[512]{0:T(512)S(1)} %copy-done.101, f32[512]{0:T(512)S(1)} %copy-done.100, f32[1152]{0:T(1024)S(1)} %copy-done.81, f32[512]{0:T(512)S(1)} %copy-done.95), kind=kOutput, calls=%fused_computation.148 | convolution fusion | flops 8157855744 | bytes 42478080 | tf_op jit(solution)/shard_map/dot_general | solution.py:76
  624.6 19.4 %fusion.91 = f32[1152,6912]{1,0:T(8,128)} fusion(bf16[512,1152]{1,0:T(8,128)(2,1)} %copy-done.11, bf16[512,6912]{1,0:T(8,128)(2,1)} %get-tuple-element.176), kind=kOutput, calls=%fused_computation.162 | convolution fusion | flops 8153726976 | bytes 40108032 | tf_op jit(solution)/shard_map/dot_general | solution.py:76
  644.0 17.8 %fusion.90 = f32[1152,6912]{1,0:T(8,128)} fusion(bf16[512,1152]{1,0:T(8,128)(2,1)S(1)} %copy-done.12, bf16[512,6912]{1,0:T(8,128)(2,1)} %get-tuple-element.177), kind=kOutput, calls=%fused_computation.161 | convolution fusion | flops 8153726976 | bytes 40108032 | tf_op jit(solution)/shard_map/dot_general | solution.py:76
  661.8 44.3 %pad_maximum_fusion = f32[1152,13824]{1,0:T(8,128)} fusion(f32[1152,6912]{1,0:T(8,128)} %fusion.91, f32[1152,6912]{1,0:T(8,128)} %fusion.90), kind=kLoop, calls=%fused_computation | loop fusion | flops 15925248 | bytes 127401984 | tf_op jit(solution)/shard_map/concatenate | solution.py:81
  707.8 15.4 reduce-scatter.13.cloned.1.call-done
  725.2 322.3 %reduce-scatter.11.cloned.1.call-done = f32[432,1152]{1,0:T(8,128)} async-done(((f32[6912,1152]{1,0:T(8,128)}), f32[432,1152]{1,0:T(8,128)}) %reduce-scatter.11.cloned.1.call-update) | async-done | bytes 1990672 | tf_op jit(solution)/shard_map/reduce_scatter | solution.py:199
  1050.1 608.0 %reduce-scatter.15.cloned.1.call-done = f32[72,13824]{1,0:T(8,128)} async-done(((f32[1152,13824]{1,0:T(8,128)}), f32[72,13824]{1,0:T(8,128)}) %reduce-scatter.15.cloned.1.call-update) | async-done | bytes 3981328
  1674.7 41.3 %all-reduce.7 = (f32[1152]{0:T(1024)}, f32[256]{0:T(256)}, f32[256]{0:T(256)}, f32[1152]{0:T(1024)}, f32[1152]{0:T(1024)}, /*index=5*/f32[1152]{0:T(1024)}) all-reduce(f32[1152]{0:T(1024)} %get-tuple-element.153, f32[256]{0:T(256)} %fusion.35, f32[256]{0:T(256)} %get-tuple-element.155, ...), channel_id=1, replica_groups=mesh['replica'=2,'fsdp'=16] {'replica','fsdp'}, use_global_device_ids=true, to_apply=%region_24.25 | all-reduce | flops 5120 | bytes 40960 | tf_op jit(solution)/shard_map/psum | solution.py:270
  1728.0 28.5 %all-reduce.12.cloned.1.call-done = (bf16[72,1536]{0,1:T(8,128)(2,1)}, bf16[72,13824]{1,0:T(8,128)(2,1)}, bf16[64,1152]{1,0:T(8,128)(2,1)}, bf16[432,1152]{1,0:T(8,128)(2,1)}) async-done(((bf16[72,1536]{0,1:T(8,128)(2,1)}, bf16[72,13824]{1,0:T(8,128)(2,1)}, bf16[64,1152]{1,0:T(8,128)(2,1)}, bf16[432,1152]{1,0:T(8,128)(2,1)}), (bf16[72,1536]{0,1:T(8,128)(2,1)}, bf16[72,13824]{1,0:T(8,128)(2,1)}, ...) | async-done | bytes 3354640 | tf_op jit(solution)/shard_map/psum | solution.py:293
  (354 shorter events, 129.0 us)
Async XLA Ops:
  7.3 72.9 %copy-start.9 = (bf16[512,1152]{1,0:T(8,128)(2,1)S(1)}, bf16[512,1152]{1,0:T(8,128)(2,1)}, u32[]{:S(2)}) copy-start(bf16[512,1152]{1,0:T(8,128)(2,1)} %param.16) | copy-start | bytes 3538948
  7.3 73.8 %copy-start.69 = (bf16[72,256]{1,0:T(8,128)(2,1)S(1)}, bf16[72,256]{1,0:T(8,128)(2,1)}, u32[]{:S(2)}) copy-start(bf16[72,256]{1,0:T(8,128)(2,1)} %param.20) | copy-start | bytes 110596
  7.3 123.2 %all-gather.6.cloned.1.call-start = ((), (), s32[]{:S(2)}) async-start(), calls=%async_computation.4 | async-start | bytes 2506752 | tf_op jit(solution)/shard_map/all_gather | solution.py:108
  8.0 140.0 %all-gather.8.cloned.1.call-start = ((), (), s32[]{:S(2)}) async-start(), calls=%async_computation.5 | async-start | bytes 2506752 | tf_op jit(solution)/shard_map/all_gather | solution.py:111
  8.8 216.8 %all-gather.10.cloned.1.call-start = ((), (), s32[]{:S(2)}) async-start(), calls=%async_computation.6 | async-start | bytes 16920576 | tf_op jit(solution)/shard_map/all_gather | solution.py:163
  9.5 337.8 %all-gather.12.cloned.1.call-start = ((), (), s32[]{:S(2)}) async-start(), calls=%async_computation.7 | async-start | bytes 16920576 | tf_op jit(solution)/shard_map/all_gather | solution.py:164
  10.1 459.0 %all-gather.14.cloned.1.call-start = ((), (), s32[]{:S(2)}) async-start(), calls=%async_computation.8 | async-start | bytes 16920576 | tf_op jit(solution)/shard_map/all_gather | solution.py:165
  10.7 695.5 %reduce-scatter.9.cloned.1.call-start = ((), (), s32[]{:S(2)}) async-start(), calls=%async_computation.9 | async-start | bytes 5013504 | tf_op jit(solution)/shard_map/reduce_scatter | solution.py:264
  78.3 25.2 %copy-start.89 = (f32[256]{0:T(256)}, f32[256]{0:T(256)S(1)}, u32[]{:S(2)}) copy-start(f32[256]{0:T(256)S(1)} %convert_element_type.116) | copy-start | bytes 3076
  78.9 51.5 %copy-start.64 = (f32[1152]{0:T(1024)}, f32[1152]{0:T(1024)S(1)}, u32[]{:S(2)}) copy-start(f32[1152]{0:T(1024)S(1)} %convert_element_type.113) | copy-start | bytes 13828
  78.9 73.4 %copy-start.62 = (f32[1152]{0:T(1024)}, f32[1152]{0:T(1024)S(1)}, u32[]{:S(2)}) copy-start(f32[1152]{0:T(1024)S(1)} %convert_element_type.123) | copy-start | bytes 13828
  80.1 24.1 %copy-start.98 = (f32[128]{0:T(128)}, f32[128]{0:T(128)S(1)}, u32[]{:S(2)}) copy-start(f32[128]{0:T(128)S(1)} %multiply_power_fusion) | copy-start | bytes 1540
  81.0 48.2 %copy-start.83 = (f32[512]{0:T(512)}, f32[512]{0:T(512)S(1)}, u32[]{:S(2)}) copy-start(f32[512]{0:T(512)S(1)} %get-tuple-element.196) | copy-start | bytes 6148
  108.0 37.3 %copy-start.29 = (pred[512,512]{0,1:T(8,128)(4,1)}, pred[512,512]{0,1:T(8,128)(4,1)S(1)}, u32[]{:S(2)}) copy-start(pred[512,512]{0,1:T(8,128)(4,1)S(1)} %fusion.52) | copy-start | bytes 786436
  153.6 87.9 %copy-start.86 = (f32[512]{0:T(512)}, f32[512]{0:T(512)S(1)}, u32[]{:S(2)}) copy-start(f32[512]{0:T(512)S(1)} %get-tuple-element.202) | copy-start | bytes 6148
  153.9 193.4 %copy-start.11 = (bf16[512,1152]{1,0:T(8,128)(2,1)}, bf16[512,1152]{1,0:T(8,128)(2,1)S(1)}, u32[]{:S(2)}) copy-start(bf16[512,1152]{1,0:T(8,128)(2,1)S(1)} %multiply_convert_fusion.2) | copy-start | bytes 3538948
  531.7 16.0 copy-start.6
  531.7 16.0 copy-start.63
  555.7 167.5 %reduce-scatter.13.cloned.1.call-start = ((), (), s32[]{:S(2)}) async-start(), calls=%async_computation.11 | async-start | bytes 7520256
  605.2 442.3 %reduce-scatter.11.cloned.1.call-start = ((), (), s32[]{:S(2)}) async-start(), calls=%async_computation.10 | async-start | bytes 33841152 | tf_op jit(solution)/shard_map/reduce_scatter | solution.py:199
  624.5 1033.6 %reduce-scatter.15.cloned.1.call-start = ((), (), s32[]{:S(2)}) async-start(), calls=%async_computation.12 | async-start | bytes 67682304
  624.6 19.4 %copy-start.12 = (bf16[512,1152]{1,0:T(8,128)(2,1)S(1)}, bf16[512,1152]{1,0:T(8,128)(2,1)}, u32[]{:S(2)}) copy-start(bf16[512,1152]{1,0:T(8,128)(2,1)} %copy-done.11) | copy-start | bytes 3538948
  706.1 1050.4 %all-reduce.12.cloned.1.call-start = ((), (), s32[]{:S(2)}) async-start(), calls=%async_computation.13 | async-start | bytes 7053312 | tf_op jit(solution)/shard_map/psum | solution.py:293
  1671.8 52.5 %copy-start.8 = (f32[512,1152]{1,0:T(8,128)S(1)}, f32[512,1152]{1,0:T(8,128)}, u32[]{:S(2)}) copy-start(f32[512,1152]{1,0:T(8,128)} %copy-done.7) | copy-start | bytes 7077892
  (96 other events, 312.2 us)
Sparse Core Ops, SparseCore 0:
  10.4 45.1 all-gather.5
  57.9 43.0 all-gather.7
  103.2 122.3 all-gather.9
  227.6 119.6 all-gather.11
  349.3 119.6 all-gather.13
  555.8 73.7 reduce-scatter.8
  634.1 89.0 reduce-scatter.12
  727.5 319.9 reduce-scatter.10
  1051.7 606.2 reduce-scatter.14
  1661.8 94.5 all-reduce.11
where the time goes:
time: 1780 us
  waiting for transfers between devices  1260 us (71%)
  matrix products  199 us (11%)
  blocking collectives  147 us (8%)
  other arithmetic  91.6 us (5%)
  local copies, waits for them, and re-layouts  64.5 us (4%)
    unnamed x12, waiting for transfers between devices  627 us
    reduce_scatter x1, waiting for transfers between devices, on_device(): lax.psum_scatter(down_term(jnp.int32(0), lax.axis_size('fsdp') * (FF // f...  322 us
    all_gather x1, waiting for transfers between devices, on_device(): lax.all_gather(w_up, 'fsdp', axis=0, tiled=True)  106 us
    all_gather x1, waiting for transfers between devices, on_device(): lax.all_gather(w_down, 'fsdp', axis=0, tiled=True)  100 us
    all_gather x1, waiting for transfers between devices, on_device(): lax.all_gather(w_gate, 'fsdp', axis=0, tiled=True)  71.6 us
    dot_general x7, matrix products, matmul_back(): lax.dot_general(left, right, (((1,), (1,)), ((), ())), preferred_element_...  66.8 us
    dot_general x7, matrix products, term(): lax.dot_general(left, right, (((0,), (0,)), ((), ())), preferred_element_...  64.7 us
    unnamed x1, blocking collectives  63.6 us
  transfers between devices with their start and end apart: 10, of which 7 were waited for; matrix products, arithmetic and copies ran while one was open for 13% of the time, Pallas kernels for 0%

commit v1 on v0

--- a/solution.py
+++ b/solution.py
@@ -267,17 +267,16 @@
         scatter_dimension=0,
         tiled=True,
     )
-    gains_all = lax.psum(
-        (
-            grad_attn_pre,
-            grad_query_gain,
-            grad_key_gain,
-            grad_attn_post,
-            grad_mlp_pre,
-            grad_mlp_post,
-        ),
-        ("replica", "fsdp"),
-    )
+    gains_all = (
+        grad_attn_pre,
+        grad_query_gain,
+        grad_key_gain,
+        grad_attn_post,
+        grad_mlp_pre,
+        grad_mlp_post,
+    )
+    for i in ("fsdp", "replica"):
+        gains_all = jax.lax.psum(gains_all, i)
     owner = lax.axis_index("fsdp")
     d_rows = D // fsdp_count
     h_rows = HD // fsdp_count

time: 1780 us -> 1780 us (level)
  blocking collectives: 147 us -> 177 us
  waiting for transfers between devices: 1260 us -> 1230 us
    psum x1 -> x2, blocking collectives: 41.3 us -> 70.8 us  [on_device(): gains_all = jax.lax.psum(gains_all, i)]
    psum x1, waiting for transfers between devices: 28.5 us -> 0.01 us  [on_device(): lax.psum(attn_in_share.astype(jnp.bfloat16), 'replica').astype(jnp.float32)]
  transfers between devices with their start and end apart: 10 -> 10, of which waited for: 7 -> 6; matrix products, arithmetic and copies ran while one was open for 13% -> 13% of each run, Pallas kernels for 0% -> 0%
where the time goes in v1:
time: 1780 us
  waiting for transfers between devices  1230 us (69%)
  matrix products  199 us (11%)
  blocking collectives  177 us (10%)
  other arithmetic  90.3 us (5%)
  local copies, waits for them, and re-layouts  63.8 us (4%)
    unnamed x12, waiting for transfers between devices  628 us
    reduce_scatter x1, waiting for transfers between devices, on_device(): lax.psum_scatter(down_term(jnp.int32(0), lax.axis_size('fsdp') * (FF // f...  322 us
    all_gather x1, waiting for transfers between devices, on_device(): lax.all_gather(w_up, 'fsdp', axis=0, tiled=True)  106 us
    all_gather x1, waiting for transfers between devices, on_device(): lax.all_gather(w_down, 'fsdp', axis=0, tiled=True)  100 us
    all_gather x1, waiting for transfers between devices, on_device(): lax.all_gather(w_gate, 'fsdp', axis=0, tiled=True)  71.7 us
    psum x2, blocking collectives, on_device(): gains_all = jax.lax.psum(gains_all, i)  70.8 us
    dot_general x7, matrix products, matmul_back(): lax.dot_general(left, right, (((1,), (1,)), ((), ())), preferred_element_...  66.8 us
    dot_general x7, matrix products, term(): lax.dot_general(left, right, (((0,), (0,)), ((), ())), preferred_element_...  64.6 us
  transfers between devices with their start and end apart: 10, of which 6 were waited for; matrix products, arithmetic and copies ran while one was open for 13% of the time, Pallas kernels for 0%

profile of v1, /device:TPU:0, one launch (start us, length us, event | category | flops | bytes accessed | tf_op | source)
XLA Modules:
  0.0 1775.8 jit_solution(15106737263367518877)
XLA Ops:
  14.8 63.6 %all-reduce.9 = (bf16[1152]{0:T(1024)(128)(2,1)S(1)}, bf16[256]{0:T(256)(128)(2,1)S(1)}, bf16[256]{0:T(256)(128)(2,1)S(1)}, bf16[1152]{0:T(1024)(128)(2,1)S(1)},...) all-reduce(bf16[1152]{0:T(1024)(128)(2,1)S(1)} %dynamic-update-slic, ...), channel_id=1, replica_groups=mesh['replica'=2,'fsdp'=16] {'fsdp'}, use_global_device_ids=true, to_apply=%add | all-reduce | flops 5120 | bytes 20480
  81.0 21.2 %all_gather.41 = bf16[1152,256]{1,0:T(8,128)(2,1)S(1)} all-gather(bf16[72,256]{1,0:T(8,128)(2,1)S(1)} %copy-done.69), channel_id=1, replica_groups=mesh['replica'=2,'fsdp'=16] {'fsdp'}, dimensions={0}, use_global_device_ids=true | all-gather | bytes 626688 | tf_op jit(solution)/shard_map/all_gather | solution.py:109
  107.9 21.2 %all_gather.40 = bf16[1152,256]{1,0:T(8,128)(2,1)S(1)} all-gather(bf16[72,256]{1,0:T(8,128)(2,1)S(1)} %copy-done.70), channel_id=1, replica_groups=mesh['replica'=2,'fsdp'=16] {'fsdp'}, dimensions={0}, use_global_device_ids=true | all-gather | bytes 626688 | tf_op jit(solution)/shard_map/all_gather | solution.py:110
  153.9 71.7 %all-gather.10.cloned.1.call-done = bf16[1152,6912]{1,0:T(8,128)(2,1)} async-done(((bf16[72,6912]{1,0:T(8,128)(2,1)}), bf16[1152,6912]{1,0:T(8,128)(2,1)}) %all-gather.10.cloned.1.call-update) | async-done | bytes 15925264 | tf_op jit(solution)/shard_map/all_gather | solution.py:163
  225.6 15.8 fusion.86
  241.4 106.0 %all-gather.12.cloned.1.call-done = bf16[1152,6912]{1,0:T(8,128)(2,1)} async-done(((bf16[72,6912]{1,0:T(8,128)(2,1)}), bf16[1152,6912]{1,0:T(8,128)(2,1)}) %all-gather.12.cloned.1.call-update) | async-done | bytes 15925264 | tf_op jit(solution)/shard_map/all_gather | solution.py:164
  347.3 21.5 %multiply_convert_fusion.1 = (bf16[512,6912]{1,0:T(8,128)(2,1)}, f32[512,6912]{1,0:T(8,128)}) fusion(f32[512,6912]{1,0:T(8,128)} %fusion.86, bf16[512,1152]{1,0:T(8,128)(2,1)S(1)} %multiply_convert_fusion.2, bf16[1152,6912]{1,0:T(8,128)(2,1)} %all-gather.12.cloned.1.call-done), kind=kOutput, calls=%fused_computation.11 | convolution fusion | flops 8189116416 | bytes 52494336 | tf_op jit(solution)/shard_map/dot_general | solution.py:63
  368.8 100.3 %all-gather.14.cloned.1.call-done = bf16[6912,1152]{1,0:T(8,128)(2,1)} async-done(((bf16[432,1152]{1,0:T(8,128)(2,1)}), bf16[6912,1152]{1,0:T(8,128)(2,1)}) %all-gather.14.cloned.1.call-update) | async-done | bytes 15925264 | tf_op jit(solution)/shard_map/all_gather | solution.py:165
  469.1 14.5 multiply_reduce_fusion.4
  487.4 28.6 %multiply_convert_fusion = (bf16[512,6912]{1,0:T(8,128)(2,1)}, bf16[512,6912]{1,0:T(8,128)(2,1)}) fusion(f32[512,6912]{1,0:T(8,128)} %fusion.86, f32[512,6912]{1,0:T(8,128)} %get-tuple-element.222, bf16[6912,1152]{1,0:T(8,128)(2,1)} %all-gather.14.cloned.1.call-done, bf16[512,1152]{1,0:T(8,128)(2,1)S(1)} %copy-done.26, f32[512,1152]{1,0:T(8,128)} %copy-done.33, ...), kind=kOutput, calls=%fused_computation.10 | convolution fusion | flops 8242790400 | bytes 61942272 | tf_op jit(solution)/shard_map/dot_general | solution.py:67
  516.0 15.7 fusion.87
  531.7 16.0 multiply_reduce_fusion
  587.4 3.9 fusion.77
  591.3 5.7 pad_maximum_fusion.1
  597.0 8.1 copy.151
  605.9 18.6 %fusion.69 = f32[6912,1152]{1,0:T(8,128)} fusion(bf16[512,6912]{1,0:T(8,128)(2,1)} %get-tuple-element.221, bf16[512,1152]{1,0:T(8,128)(2,1)} %param.17, f32[512,1152]{1,0:T(8,128)} %copy-done.33, f32[512]{0:T(512)S(1)} %copy-done.101, f32[512]{0:T(512)S(1)} %copy-done.100, f32[1152]{0:T(1024)S(1)} %copy-done.81, f32[512]{0:T(512)S(1)} %copy-done.95), kind=kOutput, calls=%fused_computation.148 | convolution fusion | flops 8157855744 | bytes 42478080 | tf_op jit(solution)/shard_map/dot_general | solution.py:76
  624.6 19.3 %fusion.91 = f32[1152,6912]{1,0:T(8,128)} fusion(bf16[512,1152]{1,0:T(8,128)(2,1)} %copy-done.11, bf16[512,6912]{1,0:T(8,128)(2,1)} %get-tuple-element.182), kind=kOutput, calls=%fused_computation.162 | convolution fusion | flops 8153726976 | bytes 40108032 | tf_op jit(solution)/shard_map/dot_general | solution.py:76
  643.9 17.9 %fusion.90 = f32[1152,6912]{1,0:T(8,128)} fusion(bf16[512,1152]{1,0:T(8,128)(2,1)S(1)} %copy-done.12, bf16[512,6912]{1,0:T(8,128)(2,1)} %get-tuple-element.183), kind=kOutput, calls=%fused_computation.161 | convolution fusion | flops 8153726976 | bytes 40108032 | tf_op jit(solution)/shard_map/dot_general | solution.py:76
  661.8 42.9 %pad_maximum_fusion = f32[1152,13824]{1,0:T(8,128)} fusion(f32[1152,6912]{1,0:T(8,128)} %fusion.91, f32[1152,6912]{1,0:T(8,128)} %fusion.90), kind=kLoop, calls=%fused_computation | loop fusion | flops 15925248 | bytes 127401984 | tf_op jit(solution)/shard_map/concatenate | solution.py:81
  706.5 16.8 reduce-scatter.13.cloned.1.call-done
  725.2 321.9 %reduce-scatter.11.cloned.1.call-done = f32[432,1152]{1,0:T(8,128)} async-done(((f32[6912,1152]{1,0:T(8,128)}), f32[432,1152]{1,0:T(8,128)}) %reduce-scatter.11.cloned.1.call-update) | async-done | bytes 1990672 | tf_op jit(solution)/shard_map/reduce_scatter | solution.py:199
  1049.7 608.0 %reduce-scatter.15.cloned.1.call-done = f32[72,13824]{1,0:T(8,128)} async-done(((f32[1152,13824]{1,0:T(8,128)}), f32[72,13824]{1,0:T(8,128)}) %reduce-scatter.15.cloned.1.call-update) | async-done | bytes 3981328
  1674.4 60.3 %all-reduce.7 = (f32[1152]{0:T(1024)}, f32[256]{0:T(256)}, f32[256]{0:T(256)}, f32[1152]{0:T(1024)}, f32[1152]{0:T(1024)}, /*index=5*/f32[1152]{0:T(1024)}) all-reduce(f32[1152]{0:T(1024)} %get-tuple-element.153, f32[256]{0:T(256)} %fusion.35, f32[256]{0:T(256)} %get-tuple-element.155, ...), channel_id=1, replica_groups=mesh['replica'=2,'fsdp'=16] {'fsdp'}, use_global_device_ids=true, to_apply=%region_24.25 | all-reduce | flops 5120 | bytes 40960 | tf_op jit(solution)/shard_map/psum | solution.py:279
  1734.7 10.5 all-reduce.8
  (355 shorter events, 128.4 us)
Async XLA Ops:
  7.3 72.9 %copy-start.9 = (bf16[512,1152]{1,0:T(8,128)(2,1)S(1)}, bf16[512,1152]{1,0:T(8,128)(2,1)}, u32[]{:S(2)}) copy-start(bf16[512,1152]{1,0:T(8,128)(2,1)} %param.16) | copy-start | bytes 3538948
  7.3 73.8 %copy-start.69 = (bf16[72,256]{1,0:T(8,128)(2,1)S(1)}, bf16[72,256]{1,0:T(8,128)(2,1)}, u32[]{:S(2)}) copy-start(bf16[72,256]{1,0:T(8,128)(2,1)} %param.20) | copy-start | bytes 110596
  7.3 123.1 %all-gather.6.cloned.1.call-start = ((), (), s32[]{:S(2)}) async-start(), calls=%async_computation.4 | async-start | bytes 2506752 | tf_op jit(solution)/shard_map/all_gather | solution.py:108
  8.0 139.9 %all-gather.8.cloned.1.call-start = ((), (), s32[]{:S(2)}) async-start(), calls=%async_computation.5 | async-start | bytes 2506752 | tf_op jit(solution)/shard_map/all_gather | solution.py:111
  8.8 216.8 %all-gather.10.cloned.1.call-start = ((), (), s32[]{:S(2)}) async-start(), calls=%async_computation.6 | async-start | bytes 16920576 | tf_op jit(solution)/shard_map/all_gather | solution.py:163
  9.5 337.8 %all-gather.12.cloned.1.call-start = ((), (), s32[]{:S(2)}) async-start(), calls=%async_computation.7 | async-start | bytes 16920576 | tf_op jit(solution)/shard_map/all_gather | solution.py:164
  10.1 459.0 %all-gather.14.cloned.1.call-start = ((), (), s32[]{:S(2)}) async-start(), calls=%async_computation.8 | async-start | bytes 16920576 | tf_op jit(solution)/shard_map/all_gather | solution.py:165
  10.7 694.1 %reduce-scatter.9.cloned.1.call-start = ((), (), s32[]{:S(2)}) async-start(), calls=%async_computation.9 | async-start | bytes 5013504 | tf_op jit(solution)/shard_map/reduce_scatter | solution.py:264
  78.3 25.1 %copy-start.89 = (f32[256]{0:T(256)}, f32[256]{0:T(256)S(1)}, u32[]{:S(2)}) copy-start(f32[256]{0:T(256)S(1)} %convert_element_type.116) | copy-start | bytes 3076
  78.9 51.4 %copy-start.64 = (f32[1152]{0:T(1024)}, f32[1152]{0:T(1024)S(1)}, u32[]{:S(2)}) copy-start(f32[1152]{0:T(1024)S(1)} %convert_element_type.113) | copy-start | bytes 13828
  79.0 73.3 %copy-start.62 = (f32[1152]{0:T(1024)}, f32[1152]{0:T(1024)S(1)}, u32[]{:S(2)}) copy-start(f32[1152]{0:T(1024)S(1)} %convert_element_type.123) | copy-start | bytes 13828
  80.2 24.0 %copy-start.98 = (f32[128]{0:T(128)}, f32[128]{0:T(128)S(1)}, u32[]{:S(2)}) copy-start(f32[128]{0:T(128)S(1)} %multiply_power_fusion) | copy-start | bytes 1540
  81.0 48.1 %copy-start.83 = (f32[512]{0:T(512)}, f32[512]{0:T(512)S(1)}, u32[]{:S(2)}) copy-start(f32[512]{0:T(512)S(1)} %get-tuple-element.202) | copy-start | bytes 6148
  107.9 37.3 %copy-start.29 = (pred[512,512]{0,1:T(8,128)(4,1)}, pred[512,512]{0,1:T(8,128)(4,1)S(1)}, u32[]{:S(2)}) copy-start(pred[512,512]{0,1:T(8,128)(4,1)S(1)} %fusion.52) | copy-start | bytes 786436
  153.6 87.8 %copy-start.86 = (f32[512]{0:T(512)}, f32[512]{0:T(512)S(1)}, u32[]{:S(2)}) copy-start(f32[512]{0:T(512)S(1)} %get-tuple-element.208) | copy-start | bytes 6148
  153.9 193.4 %copy-start.11 = (bf16[512,1152]{1,0:T(8,128)(2,1)}, bf16[512,1152]{1,0:T(8,128)(2,1)S(1)}, u32[]{:S(2)}) copy-start(bf16[512,1152]{1,0:T(8,128)(2,1)S(1)} %multiply_convert_fusion.2) | copy-start | bytes 3538948
  531.7 16.0 copy-start.6
  531.7 16.0 copy-start.63
  555.7 167.5 %reduce-scatter.13.cloned.1.call-start = ((), (), s32[]{:S(2)}) async-start(), calls=%async_computation.11 | async-start | bytes 7520256
  605.2 442.0 %reduce-scatter.11.cloned.1.call-start = ((), (), s32[]{:S(2)}) async-start(), calls=%async_computation.10 | async-start | bytes 33841152 | tf_op jit(solution)/shard_map/reduce_scatter | solution.py:199
  624.5 1033.3 %reduce-scatter.15.cloned.1.call-start = ((), (), s32[]{:S(2)}) async-start(), calls=%async_computation.12 | async-start | bytes 67682304
  624.6 19.3 %copy-start.12 = (bf16[512,1152]{1,0:T(8,128)(2,1)S(1)}, bf16[512,1152]{1,0:T(8,128)(2,1)}, u32[]{:S(2)}) copy-start(bf16[512,1152]{1,0:T(8,128)(2,1)} %copy-done.11) | copy-start | bytes 3538948
  704.7 1051.8 %all-reduce.13.cloned.1.call-start = ((), (), s32[]{:S(2)}) async-start(), calls=%async_computation.13 | async-start | bytes 7053312 | tf_op jit(solution)/shard_map/psum | solution.py:292
  1671.5 81.3 %copy-start.8 = (f32[512,1152]{1,0:T(8,128)S(1)}, f32[512,1152]{1,0:T(8,128)}, u32[]{:S(2)}) copy-start(f32[512,1152]{1,0:T(8,128)} %copy-done.7) | copy-start | bytes 7077892
  (96 other events, 312.3 us)
Sparse Core Ops, SparseCore 0:
  10.4 45.1 all-gather.5
  57.9 43.0 all-gather.7
  103.2 122.3 all-gather.9
  227.6 119.6 all-gather.11
  349.4 119.6 all-gather.13
  555.9 73.6 reduce-scatter.8
  634.1 89.1 reduce-scatter.12
  727.5 319.5 reduce-scatter.10
  1051.4 606.3 reduce-scatter.14
  1661.5 94.6 all-reduce.12
